TPU v7x, 128 devices: a whole 4x4x4 slice. The times are simulated.
128 devices in a mesh: dp: 64 (over y, z_lo, x, core), rep: 2 (over z_hi).
Axes of the slice: x: 4, y: 4, z: 4 (z_hi: 2, z_lo: 2; z = z_hi * 2 + z_lo), core: 2. Of those that a mesh axis runs over, the one named last changes fastest.
Arguments:
- queries: bfloat16 [8192, 2048], P(('dp', 'rep')), may hold values from -24 to 24
- documents: bfloat16 [8192, 2048], P(('dp', 'rep')), may hold values from -24 to 24
- partner: int32 [8192], P(('dp', 'rep')), may hold values from 0 to 8191, each once
Outputs:
- grad_queries: float32 [8192, 2048], P(('dp', 'rep'))
- grad_documents: float32 [8192, 2048], P(('dp', 'rep'))
Inputs may be any that keep to these rules, and one draw needn't show every extreme that they name: `partner`: every document index appears exactly once.
All inputs are finite; a program needn't handle non-finite values.
Results may differ from a plain program's by a relative error of at most 0.0031.
Values may be sent and summed in bfloat16 or wider, within the bound.
A program may use at most 256 MiB of HBM per device.

v0:
```python
import jax
import jax.numpy as jnp
from jax import lax
from jax.sharding import Mesh
from jax.sharding import PartitionSpec as P

WIDTHS = 9
DP = ("dp_0", "dp_1", "dp_2", "dp_3")
DP_REP = ("dp_0", "dp_1", "dp_2", "dp_3", "rep")
logit_gain = 3.0


def contract(first_op, second_op):
    return lax.dot_general(
        first_op, second_op, (((1,), (1,)), ((), ())), preferred_element_type=jnp.float32
    )


def width_list(feature_dim):
    return [feature_dim >> WIDTHS - 1 - nested for nested in range(WIDTHS)]


def scores(first_op, second_op):
    uppers = width_list(first_op.shape[1])
    result = []
    running = jnp.zeros((first_op.shape[0], second_op.shape[0]), jnp.float32)
    lower_col = 0
    for upper_col in uppers:
        running = running + contract(
            first_op[:, lower_col:upper_col], second_op[:, lower_col:upper_col]
        )
        result.append(running * (logit_gain * upper_col ** (-0.5)))
        lower_col = upper_col
    return result


def band_sums(logit_list, total_list, target, uppers):
    bands = [None] * len(uppers)
    running = None
    for nested in reversed(range(len(uppers))):
        scale = logit_gain * uppers[nested] ** (-0.5)
        weight = (jnp.exp(logit_list[nested] - total_list[nested]) - target) * scale
        running = weight if running is None else running + weight
        bands[nested] = running.astype(jnp.bfloat16)
    return bands


def spread(bands, operand, uppers, transposed):
    pieces = []
    lower_col = 0
    for nested, upper_col in enumerate(uppers):
        block_part = operand[:, lower_col:upper_col]
        if transposed:
            product = lax.dot_general(
                bands[nested],
                block_part,
                (((0,), (0,)), ((), ())),
                preferred_element_type=jnp.float32,
            )
        else:
            product = jnp.dot(bands[nested], block_part, preferred_element_type=jnp.float32)
        pieces.append(product)
        lower_col = upper_col
    return jnp.concatenate(pieces, axis=1)


Q_AXES = ("dp_0", "dp_1")
D_AXES = ("dp_2", "dp_3", "rep")


def on_device(queries, documents, partner):
    own_rows = queries.shape[0]
    uppers = width_list(queries.shape[1])
    rows = lax.all_gather(queries, Q_AXES, axis=0, tiled=True)
    row_partner = lax.all_gather(partner, Q_AXES, axis=0, tiled=True)
    docs = lax.all_gather(documents, D_AXES, axis=0, tiled=True)
    x_size, core_size, rep_size = [lax.axis_size(name) for name in D_AXES]
    block = lax.axis_index(Q_AXES)
    shards = block * (x_size * core_size * rep_size)
    col_ids = shards * own_rows + jnp.arange(docs.shape[0], dtype=jnp.int32)
    target = (row_partner[:, None] == col_ids[None, :]).astype(jnp.float32)
    logit_list = scores(rows, docs)
    row_peaks = jnp.stack([jnp.max(logits, axis=1) for logits in logit_list])
    masses = jnp.stack(
        [
            jnp.sum(jnp.exp(logits - row_peaks[nested][:, None]), axis=1)
            for nested, logits in enumerate(logit_list)
        ]
    )
    parts = lax.all_gather(row_peaks + jnp.log(masses), Q_AXES, axis=0)
    peak = jnp.max(parts, axis=0)
    totals = peak + jnp.log(jnp.sum(jnp.exp(parts - peak[None]), axis=0))
    bands = band_sums(
        logit_list, [totals[nested][:, None] for nested in range(len(uppers))], target, uppers
    )
    grad_documents = lax.psum_scatter(
        spread(bands, rows, uppers, True), D_AXES, scatter_dimension=0, tiled=True
    )
    grad_queries = lax.psum_scatter(
        spread(bands, docs, uppers, False), Q_AXES, scatter_dimension=0, tiled=True
    )
    return (grad_queries, grad_documents)


def solution(mesh):
    finer = Mesh(
        mesh.devices.reshape(4, 2, 4, 2, mesh.shape["rep"]), ("dp_0", "dp_1", "dp_2", "dp_3", "rep")
    )
    placed = (P(DP_REP, None), P(DP_REP, None), P(DP_REP))
    return jax.shard_map(
        on_device,
        mesh=finer,
        in_specs=placed,
        out_specs=(P(DP_REP, None), P(DP_REP, None)),
        check_vma=False,
    )
```

profile of v0, /device:TPU:0, one launch (start us, length us, event | category | flops | bytes accessed | tf_op | source)
XLA Modules:
  0.0 406.1 jit_solution(15997544416432338773)
XLA Ops:
  7.2 0.7 all-gather.3.cloned.1.call-update
  7.9 0.7 all-gather.5.cloned.1.call-update
  8.7 1.2 dynamic-slice
  10.6 0.9 dynamic-update-slice
  11.5 12.0 %all-reduce = s32[512]{0:T(512)S(1)} all-reduce(s32[512]{0:T(512)S(1)} %dynamic-update-slice), channel_id=1, replica_groups=mesh['dp_0'=4,'dp_1'=2,'dp_2'=4,'dp_3'=2,'rep'=2] {'dp_0','dp_1'}, use_global_device_ids=true, to_apply=%add | all-reduce | flops 512 | bytes 4096
  23.5 39.8 %all-gather.3.cloned.1.call-done = bf16[512,2048]{1,0:T(8,128)(2,1)} async-done(((bf16[64,2048]{1,0:T(8,128)(2,1)}), bf16[512,2048]{1,0:T(8,128)(2,1)}) %all-gather.3.cloned.1.call-update) | async-done | bytes 2097168 | tf_op jit(solution)/shard_map/all_gather | solution.py:74
  63.3 59.5 %all-gather.5.cloned.1.call-done = bf16[1024,2048]{1,0:T(8,128)(2,1)} async-done(((bf16[64,2048]{1,0:T(8,128)(2,1)}), bf16[1024,2048]{1,0:T(8,128)(2,1)}) %all-gather.5.cloned.1.call-update) | async-done | bytes 4194320 | tf_op jit(solution)/shard_map/all_gather | solution.py:76
  122.8 1.5 multiply_reduce_fusion.7
  124.3 0.5 exponential_reduce_fusion.8
  124.8 1.6 multiply_reduce_fusion.6
  126.5 0.5 exponential_reduce_fusion.7
  127.0 1.8 multiply_reduce_fusion.5
  128.8 0.5 exponential_reduce_fusion.6
  129.3 1.8 multiply_reduce_fusion.4
  131.2 0.5 exponential_reduce_fusion.5
  131.7 1.8 multiply_reduce_fusion.3
  133.5 0.5 exponential_reduce_fusion.4
  134.1 1.7 multiply_reduce_fusion.2
  135.8 0.5 exponential_reduce_fusion.3
  136.3 1.9 multiply_reduce_fusion.1
  138.2 0.5 exponential_reduce_fusion.2
  138.7 2.4 multiply_reduce_fusion
  141.2 0.5 exponential_reduce_fusion.1
  141.7 3.5 fusion.92
  145.2 1.4 copy-done.16
  147.2 28.6 %all_gather.15 = f32[8,9,512]{2,1,0:T(8,128)S(1)} all-gather(f32[1,9,512]{2,1,0:T(8,128)S(1)} %log_add_fusion.1), channel_id=1, replica_groups=mesh['dp_0'=4,'dp_1'=2,'dp_2'=4,'dp_3'=2,'rep'=2] {'dp_0','dp_1'}, dimensions={0}, use_global_device_ids=true | all-gather | bytes 165888 | tf_op jit(solution)/shard_map/all_gather | solution.py:90
  176.0 9.6 %fusion.17 = (bf16[512,1024]{1,0:T(8,128)(2,1)S(1)}, bf16[512,1024]{1,0:T(8,128)(2,1)S(1)}, bf16[512,1024]{1,0:T(8,128)(2,1)S(1)}, bf16[512,1024]{1,0:T(8,128)(2...) fusion(f32[512,1024]{1,0:T(8,128)S(1)} %get-tuple-element.24, ...), kind=kLoop, calls=%fused_computation.27 | loop fusion | flops 27787264 | bytes 27287552 | tf_op jit(solution)/shard_map/convert_element_type | solution.py:44
  185.8 1.4 fusion.18
  187.6 1.2 fusion.48
  188.9 1.2 fusion.45
  190.1 1.2 fusion.42
  191.3 1.2 fusion.39
  192.6 1.2 fusion.36
  193.7 1.2 fusion.33
  195.0 1.7 fusion.27
  196.7 5.9 %concatenate.20 = f32[512,2048]{1,0:T(8,128)} concatenate(f32[512,8]{1,0:T(8,128)S(1)} %fusion.66, f32[512,8]{1,0:T(8,128)} %fusion.48, f32[512,16]{1,0:T(8,128)} %fusion.45, f32[512,32]{1,0:T(8,128)} %fusion.42, f32[512,64]{1,0:T(8,128)} %fusion.39, f32[512,128]{1,0:T(8,128)} %fusion.36, f32[512,256]{1,0:T(8,128)} %fusion.33, f32[512,512]{1,0:T(8,128)} %fusion.27, ...), dimensions={1} | concatenate | bytes 8388608 | tf_op jit(solution)/shard_map/concatenate | solution.py:64
  202.7 2.3 convolution_dynamic-update-slice_fusion.8
  205.0 2.0 convolution_dynamic-update-slice_fusion.7
  206.9 2.0 convolution_dynamic-update-slice_fusion.6
  208.9 1.0 convolution_dynamic-update-slice_fusion.5
  209.9 1.1 convolution_dynamic-update-slice_fusion.4
  211.0 1.2 convolution_dynamic-update-slice_fusion.3
  212.2 1.5 convolution_dynamic-update-slice_fusion.2
  213.8 2.1 convolution_dynamic-update-slice_fusion.1
  215.8 3.5 convolution_dynamic-update-slice_fusion
  219.4 9.1 %copy.31 = f32[1024,2048]{1,0:T(8,128)} copy(f32[1024,2048]{0,1:T(8,128)} %convolution_dynamic-update-slice_fusion) | data formatting | bytes 16777216
  228.5 62.8 %reduce-scatter.5.cloned.1.call-done = f32[64,2048]{1,0:T(8,128)} async-done(((f32[512,2048]{1,0:T(8,128)}), f32[64,2048]{1,0:T(8,128)}) %reduce-scatter.5.cloned.1.call-update) | async-done | bytes 524304 | tf_op jit(solution)/shard_map/reduce_scatter | solution.py:99
  291.4 108.2 %reduce-scatter.7.cloned.1.call-done = f32[64,2048]{1,0:T(8,128)} async-done(((f32[1024,2048]{1,0:T(8,128)}), f32[64,2048]{1,0:T(8,128)}) %reduce-scatter.7.cloned.1.call-update) | async-done | bytes 524304
  (66 shorter events, 1.5 us)
Async XLA Ops:
  7.2 56.1 %all-gather.3.cloned.1.call-start = ((), (), s32[]{:S(2)}) async-start(), calls=%async_computation.2 | async-start | bytes 2359296 | tf_op jit(solution)/shard_map/all_gather | solution.py:74
  7.9 114.9 %all-gather.5.cloned.1.call-start = ((), (), s32[]{:S(2)}) async-start(), calls=%async_computation.3 | async-start | bytes 4456448 | tf_op jit(solution)/shard_map/all_gather | solution.py:76
  8.6 282.7 %reduce-scatter.5.cloned.1.call-start = ((), (), s32[]{:S(2)}) async-start(), calls=%async_computation.4 | async-start | bytes 4718592 | tf_op jit(solution)/shard_map/reduce_scatter | solution.py:99
  126.5 2.4 copy-start
  128.8 2.3 copy-start.1
  131.2 2.4 copy-start.2
  133.5 2.3 copy-start.3
  135.8 2.4 copy-start.4
  138.2 3.0 copy-start.5
  141.2 4.0 copy-start.6
  145.2 1.4 copy-start.16
  176.0 9.7 %copy-start.17 = (f32[512,1024]{1,0:T(8,128)S(1)}, f32[512,1024]{1,0:T(8,128)}, u32[]{:S(2)}) copy-start(f32[512,1024]{1,0:T(8,128)} %copy-done.16) | copy-start | bytes 6291460
  176.0 9.7 %copy-start.19 = (bf16[1024,2048]{1,0:T(8,128)(2,1)S(1)}, bf16[1024,2048]{1,0:T(8,128)(2,1)}, u32[]{:S(2)}) copy-start(bf16[1024,2048]{1,0:T(8,128)(2,1)} %all-gather.5.cloned.1.call-done) | copy-start | bytes 12582916
  185.7 1.5 copy-start.15
  185.7 1.9 copy-start.13
  185.7 3.2 copy-start.11
  185.7 5.6 %copy-start.9 = (bf16[512,1024]{1,0:T(8,128)(2,1)}, bf16[512,1024]{1,0:T(8,128)(2,1)S(1)}, u32[]{:S(2)}) copy-start(bf16[512,1024]{1,0:T(8,128)(2,1)S(1)} %get-tuple-element.10) | copy-start | bytes 3145732
  185.7 6.8 %copy-start.7 = (bf16[512,1024]{1,0:T(8,128)(2,1)}, bf16[512,1024]{1,0:T(8,128)(2,1)S(1)}, u32[]{:S(2)}) copy-start(bf16[512,1024]{1,0:T(8,128)(2,1)S(1)} %get-tuple-element.11) | copy-start | bytes 3145732
  185.7 8.0 %copy-start.23 = (bf16[512,1024]{1,0:T(8,128)(2,1)}, bf16[512,1024]{1,0:T(8,128)(2,1)S(1)}, u32[]{:S(2)}) copy-start(bf16[512,1024]{1,0:T(8,128)(2,1)S(1)} %get-tuple-element.12) | copy-start | bytes 3145732
  185.7 9.2 %copy-start.21 = (bf16[512,1024]{1,0:T(8,128)(2,1)}, bf16[512,1024]{1,0:T(8,128)(2,1)S(1)}, u32[]{:S(2)}) copy-start(bf16[512,1024]{1,0:T(8,128)(2,1)S(1)} %get-tuple-element.13) | copy-start | bytes 3145732
  202.6 2.4 copy-start.14
  202.6 4.3 %copy-start.12 = (bf16[512,1024]{1,0:T(8,128)(2,1)S(1)}, bf16[512,1024]{1,0:T(8,128)(2,1)}, u32[]{:S(2)}) copy-start(bf16[512,1024]{1,0:T(8,128)(2,1)} %copy-done.11) | copy-start | bytes 3145732
  202.6 197.0 %reduce-scatter.7.cloned.1.call-start = ((), (), s32[]{:S(2)}) async-start(), calls=%async_computation.5 | async-start | bytes 8912896
  202.7 6.2 %copy-start.20 = (bf16[512,2048]{1,0:T(8,128)(2,1)S(1)}, bf16[512,2048]{1,0:T(8,128)(2,1)}, u32[]{:S(2)}) copy-start(bf16[512,2048]{1,0:T(8,128)(2,1)} %all-gather.3.cloned.1.call-done) | copy-start | bytes 6291460
  205.0 5.0 %copy-start.10 = (bf16[512,1024]{1,0:T(8,128)(2,1)S(1)}, bf16[512,1024]{1,0:T(8,128)(2,1)}, u32[]{:S(2)}) copy-start(bf16[512,1024]{1,0:T(8,128)(2,1)} %copy-done.9) | copy-start | bytes 3145732
  206.9 4.1 %copy-start.8 = (bf16[512,1024]{1,0:T(8,128)(2,1)S(1)}, bf16[512,1024]{1,0:T(8,128)(2,1)}, u32[]{:S(2)}) copy-start(bf16[512,1024]{1,0:T(8,128)(2,1)} %copy-done.7) | copy-start | bytes 3145732
  208.9 3.3 copy-start.24
  211.0 2.7 copy-start.22
  213.8 2.1 copy-start.18
Sparse Core Ops, SparseCore 0:
  9.6 53.6 all-gather.2
  65.7 57.0 all-gather.4
  202.7 88.5 reduce-scatter.4
  296.1 103.3 reduce-scatter.6
where the time goes:
time: 407 us; the launch traced here: 406 us
  waiting for transfers between devices  272 us (67%)
  matrix products  45.7 us (11%)
  blocking collectives  40.7 us (10%)
  local copies, waits for them, and re-layouts  18.8 us (5%)
  between operations  14.7 us (4%)
  other arithmetic  14.4 us (4%)
    unnamed x5, waiting for transfers between devices  110 us
    reduce_scatter x1, waiting for transfers between devices, on_device(): lax.psum_scatter(spread(bands, docs, uppers, False), Q_AXES, scatter_dime...  62.8 us
    all_gather x1, waiting for transfers between devices, on_device(): docs = lax.all_gather(documents, D_AXES, axis=0, tiled=True)  59.5 us
    all_gather x1, waiting for transfers between devices, on_device(): rows = lax.all_gather(queries, Q_AXES, axis=0, tiled=True)  39.8 us
    all_gather x1, blocking collectives, on_device(): parts = lax.all_gather(row_peaks + jnp.log(masses), Q_AXES, axis=0)  28.6 us
    dot_general x9, matrix products, contract(): lax.dot_general(first_op, second_op, (((1,), (1,)), ((), ())), preferred_...  18.1 us
    dot_general x9, matrix products, spread(): lax.dot_general(bands[nested], block_part, (((0,), (0,)), ((), ())), pref...  16.7 us
    unnamed x54, local copies, waits for them, and re-layouts  12.7 us
  transfers between devices with their start and end apart: 4, of which 4 were waited for; matrix products, arithmetic and copies ran while one was open for 7% of the time, Pallas kernels for 0%

commit v1 on v0

--- a/solution.py
+++ b/solution.py
@@ -71,7 +71,9 @@
 def on_device(queries, documents, partner):
     own_rows = queries.shape[0]
     uppers = width_list(queries.shape[1])
-    rows = lax.all_gather(queries, Q_AXES, axis=0, tiled=True)
+    rows = jnp.concatenate(
+        lax.all_to_all(jnp.stack([queries] * lax.axis_size(Q_AXES)), Q_AXES, 0, 0), axis=0
+    )
     row_partner = lax.all_gather(partner, Q_AXES, axis=0, tiled=True)
     docs = lax.all_gather(documents, D_AXES, axis=0, tiled=True)
     x_size, core_size, rep_size = [lax.axis_size(name) for name in D_AXES]

time: 407 us -> 367 us (0.902)
  waiting for transfers between devices: 272 us -> 202 us
  blocking collectives: 40.7 us -> 62.1 us
  starting transfers between devices: 0.16 us -> 6.18 us
    all_gather x1 -> x0, waiting for transfers between devices: 39.8 us -> none  [on_device(): rows = lax.all_gather(queries, Q_AXES, axis=0, tiled=True)]
    all_gather x1, waiting for transfers between devices: 59.5 us -> 30.7 us  [on_device(): docs = lax.all_gather(documents, D_AXES, axis=0, tiled=True)]
    unnamed x1, blocking collectives: 12 us -> 33.5 us
    all_to_all x0 -> x1, starting transfers between devices: none -> 6.07 us  [on_device(): lax.all_to_all(jnp.stack([queries] * lax.axis_size(Q_AXES)), Q_AXES, 0, 0)]
    unnamed x5 -> x4, waiting for transfers between devices: 110 us -> 109 us
    unnamed x54 -> x58, local copies, waits for them, and re-layouts: 12.7 us -> 13 us
  transfers between devices with their start and end apart: 4 -> 4, of which waited for: 4 -> 3; matrix products, arithmetic and copies ran while one was open for 7% -> 8% of each run, Pallas kernels for 0% -> 0%
where the time goes in v1:
time: 367 us; the launch traced here: 366 us
  waiting for transfers between devices  202 us (55%)
  blocking collectives  62.1 us (17%)
  matrix products  44.9 us (12%)
  local copies, waits for them, and re-layouts  21.5 us (6%)
  between operations  14.7 us (4%)
  other arithmetic  14.4 us (4%)
  starting transfers between devices  6.18 us (2%)
    unnamed x4, waiting for transfers between devices  109 us
    reduce_scatter x1, waiting for transfers between devices, on_device(): lax.psum_scatter(spread(bands, docs, uppers, False), Q_AXES, scatter_dime...  62.1 us
    unnamed x1, blocking collectives  33.5 us
    all_gather x1, waiting for transfers between devices, on_device(): docs = lax.all_gather(documents, D_AXES, axis=0, tiled=True)  30.7 us
    all_gather x1, blocking collectives, on_device(): parts = lax.all_gather(row_peaks + jnp.log(masses), Q_AXES, axis=0)  28.6 us
    dot_general x9, matrix products, contract(): lax.dot_general(first_op, second_op, (((1,), (1,)), ((), ())), preferred_...  18.1 us
    dot_general x9, matrix products, spread(): lax.dot_general(bands[nested], block_part, (((0,), (0,)), ((), ())), pref...  15.9 us
    unnamed x58, local copies, waits for them, and re-layouts  13 us
  transfers between devices with their start and end apart: 4, of which 3 were waited for; matrix products, arithmetic and copies ran while one was open for 8% of the time, Pallas kernels for 0%

profile of v1, /device:TPU:0, one launch (start us, length us, event | category | flops | bytes accessed | tf_op | source)
XLA Modules:
  0.0 365.7 jit_solution(12937167340569117422)
XLA Ops:
  7.2 0.7 all-gather.2.cloned.1.call-update
  7.9 2.5 stack.71
  10.4 6.1 %all-to-all-start = ((bf16[8,64,2048]{2,1,0:T(8,128)(2,1)}), bf16[8,64,2048]{2,1,0:T(8,128)(2,1)S(1)}, u32[]{:S(2)}, u32[]{:S(2)}) async-start(bf16[8,64,2048]{2,1,0:T(8,128)(2,1)} %stack.71), calls=%async_computation | async-start | bytes 4194304 | tf_op jit(solution)/shard_map/all_to_all | solution.py:75
  16.6 0.6 dynamic-slice
  18.1 33.5 %all-reduce = s32[512]{0:T(512)S(1)} all-reduce(s32[512]{0:T(512)S(1)} %dynamic-update-slice), channel_id=1, replica_groups=mesh['dp_0'=4,'dp_1'=2,'dp_2'=4,'dp_3'=2,'rep'=2] {'dp_0','dp_1'}, use_global_device_ids=true, to_apply=%add | all-reduce | flops 512 | bytes 4096
  51.6 30.7 %all-gather.2.cloned.1.call-done = bf16[1024,2048]{1,0:T(8,128)(2,1)} async-done(((bf16[64,2048]{1,0:T(8,128)(2,1)}), bf16[1024,2048]{1,0:T(8,128)(2,1)}) %all-gather.2.cloned.1.call-update) | async-done | bytes 4194320 | tf_op jit(solution)/shard_map/all_gather | solution.py:78
  82.2 1.5 multiply_reduce_fusion.7
  83.8 0.5 exponential_reduce_fusion.8
  84.3 1.6 multiply_reduce_fusion.6
  85.9 0.5 exponential_reduce_fusion.7
  86.5 1.8 multiply_reduce_fusion.5
  88.3 0.5 exponential_reduce_fusion.6
  88.8 1.8 multiply_reduce_fusion.4
  90.7 0.5 exponential_reduce_fusion.5
  91.2 1.8 multiply_reduce_fusion.3
  93.0 0.5 exponential_reduce_fusion.4
  93.5 1.7 multiply_reduce_fusion.2
  95.3 0.5 exponential_reduce_fusion.3
  95.8 1.9 multiply_reduce_fusion.1
  97.7 0.5 exponential_reduce_fusion.2
  98.2 2.4 multiply_reduce_fusion
  100.7 0.5 exponential_reduce_fusion.1
  101.2 3.5 fusion.92
  104.7 1.4 copy-done.17
  106.7 28.6 %all_gather.11 = f32[8,9,512]{2,1,0:T(8,128)S(1)} all-gather(f32[1,9,512]{2,1,0:T(8,128)S(1)} %log_add_fusion.1), channel_id=1, replica_groups=mesh['dp_0'=4,'dp_1'=2,'dp_2'=4,'dp_3'=2,'rep'=2] {'dp_0','dp_1'}, dimensions={0}, use_global_device_ids=true | all-gather | bytes 165888 | tf_op jit(solution)/shard_map/all_gather | solution.py:92
  135.5 9.6 %fusion.17 = (bf16[512,1024]{1,0:T(8,128)(2,1)S(1)}, bf16[512,1024]{1,0:T(8,128)(2,1)S(1)}, bf16[512,1024]{1,0:T(8,128)(2,1)S(1)}, bf16[512,1024]{1,0:T(8,128)(2...) fusion(f32[512,1024]{1,0:T(8,128)S(1)} %get-tuple-element.24, ...), kind=kLoop, calls=%fused_computation.27 | loop fusion | flops 27787264 | bytes 27287552 | tf_op jit(solution)/shard_map/convert_element_type | solution.py:44
  145.2 1.4 fusion.18
  147.1 1.2 fusion.48
  148.3 1.2 fusion.45
  149.5 1.2 fusion.42
  150.8 1.2 fusion.39
  152.0 1.2 fusion.36
  153.2 1.2 fusion.33
  154.4 1.7 fusion.27
  156.1 5.9 %concatenate.20 = f32[512,2048]{1,0:T(8,128)} concatenate(f32[512,8]{1,0:T(8,128)S(1)} %fusion.66, f32[512,8]{1,0:T(8,128)} %fusion.48, f32[512,16]{1,0:T(8,128)} %fusion.45, f32[512,32]{1,0:T(8,128)} %fusion.42, f32[512,64]{1,0:T(8,128)} %fusion.39, f32[512,128]{1,0:T(8,128)} %fusion.36, f32[512,256]{1,0:T(8,128)} %fusion.33, f32[512,512]{1,0:T(8,128)} %fusion.27, ...), dimensions={1} | concatenate | bytes 8388608 | tf_op jit(solution)/shard_map/concatenate | solution.py:64
  162.1 1.5 copy-done.8
  163.6 2.2 convolution_dynamic-update-slice_fusion.8
  165.8 2.3 convolution_dynamic-update-slice_fusion.7
  168.1 1.0 convolution_dynamic-update-slice_fusion.6
  169.1 1.0 convolution_dynamic-update-slice_fusion.5
  170.1 1.1 convolution_dynamic-update-slice_fusion.4
  171.2 1.2 convolution_dynamic-update-slice_fusion.3
  172.4 1.5 convolution_dynamic-update-slice_fusion.2
  174.0 2.0 convolution_dynamic-update-slice_fusion.1
  176.0 3.5 convolution_dynamic-update-slice_fusion
  179.5 9.1 %copy.31 = f32[1024,2048]{1,0:T(8,128)} copy(f32[1024,2048]{0,1:T(8,128)} %convolution_dynamic-update-slice_fusion) | data formatting | bytes 16777216
  188.7 62.1 %reduce-scatter.5.cloned.1.call-done = f32[64,2048]{1,0:T(8,128)} async-done(((f32[512,2048]{1,0:T(8,128)}), f32[64,2048]{1,0:T(8,128)}) %reduce-scatter.5.cloned.1.call-update) | async-done | bytes 524304 | tf_op jit(solution)/shard_map/reduce_scatter | solution.py:101
  250.8 108.4 %reduce-scatter.7.cloned.1.call-done = f32[64,2048]{1,0:T(8,128)} async-done(((f32[1024,2048]{1,0:T(8,128)}), f32[64,2048]{1,0:T(8,128)}) %reduce-scatter.7.cloned.1.call-update) | async-done | bytes 524304
  (70 shorter events, 1.7 us)
Async XLA Ops:
  7.2 75.1 %all-gather.2.cloned.1.call-start = ((), (), s32[]{:S(2)}) async-start(), calls=%async_computation.3 | async-start | bytes 4456448 | tf_op jit(solution)/shard_map/all_gather | solution.py:78
  10.4 6.1 %copy-start.26 = (u32[128]{0:T(128)S(1)}, u32[128]{0:T(128)}, u32[]{:S(2)}) copy-start(u32[128]{0:T(128)} %constant.45) | copy-start | bytes 1540
  10.4 7.4 %copy-start.25 = (s32[64]{0:T(128)S(1)}, s32[64]{0:T(128)}, u32[]{:S(2)}) copy-start(s32[64]{0:T(128)} %param.5) | copy-start | bytes 772
  10.4 41.1 %all-to-all-start = ((bf16[8,64,2048]{2,1,0:T(8,128)(2,1)}), bf16[8,64,2048]{2,1,0:T(8,128)(2,1)S(1)}, u32[]{:S(2)}, u32[]{:S(2)}) async-start(bf16[8,64,2048]{2,1,0:T(8,128)(2,1)} %stack.71), calls=%async_computation | async-start | bytes 4194304 | tf_op jit(solution)/shard_map/all_to_all | solution.py:75
  16.5 234.3 %reduce-scatter.5.cloned.1.call-start = ((), (), s32[]{:S(2)}) async-start(), calls=%async_computation.4 | async-start | bytes 4718592 | tf_op jit(solution)/shard_map/reduce_scatter | solution.py:101
  51.6 30.7 %copy-start.7 = (bf16[8,64,2048]{2,1,0:T(8,128)(2,1)}, bf16[8,64,2048]{2,1,0:T(8,128)(2,1)S(1)}, u32[]{:S(2)}) copy-start(bf16[8,64,2048]{2,1,0:T(8,128)(2,1)S(1)} %all-to-all-done) | copy-start | bytes 6291460
  85.9 2.4 copy-start
  88.3 2.4 copy-start.1
  90.7 2.3 copy-start.2
  93.0 2.3 copy-start.3
  95.3 2.4 copy-start.4
  97.7 3.0 copy-start.5
  100.6 4.0 %copy-start.6 = (f32[512,1024]{1,0:T(8,128)}, f32[512,1024]{1,0:T(8,128)S(1)}, u32[]{:S(2)}) copy-start(f32[512,1024]{1,0:T(8,128)S(1)} %get-tuple-element.38) | copy-start | bytes 6291460
  104.7 1.4 copy-start.17
  135.5 9.7 %copy-start.18 = (f32[512,1024]{1,0:T(8,128)S(1)}, f32[512,1024]{1,0:T(8,128)}, u32[]{:S(2)}) copy-start(f32[512,1024]{1,0:T(8,128)} %copy-done.17) | copy-start | bytes 6291460
  135.5 9.7 %copy-start.20 = (bf16[1024,2048]{1,0:T(8,128)(2,1)S(1)}, bf16[1024,2048]{1,0:T(8,128)(2,1)}, u32[]{:S(2)}) copy-start(bf16[1024,2048]{1,0:T(8,128)(2,1)} %all-gather.2.cloned.1.call-done) | copy-start | bytes 12582916
  145.2 1.5 copy-start.16
  145.2 1.9 copy-start.15
  145.2 3.2 copy-start.13
  145.2 5.6 %copy-start.11 = (bf16[512,1024]{1,0:T(8,128)(2,1)}, bf16[512,1024]{1,0:T(8,128)(2,1)S(1)}, u32[]{:S(2)}) copy-start(bf16[512,1024]{1,0:T(8,128)(2,1)S(1)} %get-tuple-element.10) | copy-start | bytes 3145732
  145.2 6.8 %copy-start.9 = (bf16[512,1024]{1,0:T(8,128)(2,1)}, bf16[512,1024]{1,0:T(8,128)(2,1)S(1)}, u32[]{:S(2)}) copy-start(bf16[512,1024]{1,0:T(8,128)(2,1)S(1)} %get-tuple-element.11) | copy-start | bytes 3145732
  145.2 7.9 %copy-start.23 = (bf16[512,1024]{1,0:T(8,128)(2,1)}, bf16[512,1024]{1,0:T(8,128)(2,1)S(1)}, u32[]{:S(2)}) copy-start(bf16[512,1024]{1,0:T(8,128)(2,1)S(1)} %get-tuple-element.12) | copy-start | bytes 3145732
  145.2 9.2 %copy-start.21 = (bf16[512,1024]{1,0:T(8,128)(2,1)}, bf16[512,1024]{1,0:T(8,128)(2,1)S(1)}, u32[]{:S(2)}) copy-start(bf16[512,1024]{1,0:T(8,128)(2,1)S(1)} %get-tuple-element.13) | copy-start | bytes 3145732
  162.0 1.6 copy-start.8
  162.1 197.1 %reduce-scatter.7.cloned.1.call-start = ((), (), s32[]{:S(2)}) async-start(), calls=%async_computation.5 | async-start | bytes 8912896
  163.6 4.5 %copy-start.14 = (bf16[512,1024]{1,0:T(8,128)(2,1)S(1)}, bf16[512,1024]{1,0:T(8,128)(2,1)}, u32[]{:S(2)}) copy-start(bf16[512,1024]{1,0:T(8,128)(2,1)} %copy-done.13) | copy-start | bytes 3145732
  165.8 4.3 %copy-start.12 = (bf16[512,1024]{1,0:T(8,128)(2,1)S(1)}, bf16[512,1024]{1,0:T(8,128)(2,1)}, u32[]{:S(2)}) copy-start(bf16[512,1024]{1,0:T(8,128)(2,1)} %copy-done.11) | copy-start | bytes 3145732
  168.1 3.1 copy-start.10
  169.1 3.3 copy-start.24
  171.2 2.7 copy-start.22
  173.9 2.0 copy-start.19
Sparse Core Ops, SparseCore 0:
  10.4 71.7 all-gather.1
  162.2 88.5 reduce-scatter.4
  255.7 103.4 reduce-scatter.6
